TPU v7x, 256 devices: a whole 4x4x8 slice. The times are simulated.
256 devices in a mesh: ep: 128 (over z, x, y), half: 2 (over core).
Axes of the slice: x: 4, y: 4, z: 8, core: 2. Of those that a mesh axis runs over, the one named last changes fastest.
Arguments:
- tokens: bfloat16 [16384, 2048], P('ep', 'half'), may hold values from -6 to 6
- gate_weights: float32 [16384, 8], P('ep'), may hold values from 0.05 to 0.3
- expert_ids: int32 [16384, 8], P('ep'), may hold values from 0 to 127, all different within a row; in each aligned block of 128 rows (0 to 127, 128 to 255, ...) at most 10 rows name the same one
- w_gate: bfloat16 [128, 2048, 768], P('ep', None, 'half'), may hold values from -0.125 to 0.125
- w_up: bfloat16 [128, 2048, 768], P('ep', None, 'half'), may hold values from -0.125 to 0.125
- w_down: bfloat16 [128, 768, 2048], P('ep', 'half'), may hold values from -0.21875 to 0.21875
Outputs:
- mixed: bfloat16 [16384, 2048], P('ep', 'half')
Inputs may be any that keep to these rules, and one draw needn't show every extreme that they name: `expert_ids`: each row names 8 different experts. Within the rows of one device (aligned blocks of 128 rows) no expert is named by more than 10 rows, and in every draw some expert is named by exactly 10 rows of some block.
All inputs are finite; a program needn't handle non-finite values.
Results may differ from a plain program's by a relative error of at most 0.0085.
Values may be sent and summed in bfloat16 or wider, within the bound.
A program may use at most 64 MiB of HBM per device.

v0:
```python
import jax
import jax.numpy as jnp
from jax import lax
from jax.sharding import PartitionSpec as P


def cut_along(value, dim, size):
    lengths = value.shape
    blocks = value.reshape(*lengths[:dim], size, lengths[dim] // size, *lengths[dim + 1 :])
    return jnp.moveaxis(blocks, dim, 0)


def summed_on_arrival(value, axis, dim):
    size = lax.axis_size(axis)
    blocks = lax.all_to_all(cut_along(value, dim, size), axis, 0, 0, tiled=True)
    return jnp.sum(blocks.astype(jnp.float32), axis=0)


def local(tokens, gate_weights, expert_ids, w_gate, w_up, w_down):
    tok_dev, half_width = tokens.shape
    top = expert_ids.shape[1]
    local_experts = w_gate.shape[0]
    experts = local_experts * lax.axis_size("ep")
    capacity = min(tok_dev, max(2, 5 * tok_dev * top // (4 * experts)))
    flat_ids = expert_ids.reshape(-1)
    columns = jnp.arange(experts, dtype=jnp.int32)
    onehot = (flat_ids[:, None] == columns[None, :]).astype(jnp.int32)
    ranks = jnp.sum((jnp.cumsum(onehot, axis=0) - onehot) * onehot, axis=1)
    slot = flat_ids * capacity + ranks
    token_of_pair = jnp.arange(tok_dev * top, dtype=jnp.int32) // top
    token_table = jnp.zeros((experts * capacity,), jnp.int32).at[slot].set(token_of_pair)
    filled = (
        jnp.zeros((experts * capacity,), jnp.bfloat16)
        .at[slot]
        .set(jnp.ones((tok_dev * top,), jnp.bfloat16))
    )
    outgoing = (tokens[token_table] * filled[:, None]).reshape(experts, capacity, half_width)
    received = lax.all_to_all(outgoing, "ep", split_axis=0, concat_axis=0, tiled=True)
    count = received.shape[1]
    whole = lax.all_gather(received, "half", axis=2, tiled=True)
    width = whole.shape[2]
    grouped = whole.reshape(-1, local_experts, count, width)
    gate = jnp.einsum("secd,edf->secf", grouped, w_gate, preferred_element_type=jnp.float32)
    up = jnp.einsum("secd,edf->secf", grouped, w_up, preferred_element_type=jnp.float32)
    hidden = (jax.nn.silu(gate) * up).astype(jnp.bfloat16)
    partial_out = jnp.einsum("secf,efd->secd", hidden, w_down, preferred_element_type=jnp.float32)
    partial_out = partial_out.astype(jnp.bfloat16).reshape(experts, count, width)
    widened = lax.optimization_barrier(partial_out).astype(jnp.float32)
    summed = summed_on_arrival(widened.astype(jnp.bfloat16), "half", 2).astype(jnp.bfloat16)
    answer = lax.all_to_all(summed, "ep", split_axis=0, concat_axis=0, tiled=True)
    picked = answer.reshape(experts * capacity, -1)[slot].reshape(tok_dev, top, -1)
    slot_out = picked.astype(jnp.float32)
    mixed = jnp.einsum("tk,tkx->tx", gate_weights, slot_out)
    return mixed.astype(jnp.bfloat16)


def solution(mesh):
    placed = (
        P("ep", "half"),
        P("ep", None),
        P("ep", None),
        P("ep", None, "half"),
        P("ep", None, "half"),
        P("ep", "half", None),
    )
    return jax.shard_map(
        local, mesh=mesh, in_specs=placed, out_specs=P("ep", "half"), check_vma=False
    )
```

profile of v0, /device:TPU:24, one launch (start us, length us, event | category | flops | bytes accessed | tf_op | source)
XLA Modules:
  0.0 341.7 jit_solution(1037426813920486707)
XLA Ops:
  6.5 0.9 copy.24
  7.6 0.7 broadcast_multiply_fusion.1
  8.4 0.2 fusion.17
  9.1 0.4 fusion.16
  9.4 4.3 %scatter_custom_fusion = s32[1280]{0:T(1024)S(1)} fusion(s32[1024]{0:T(1024)S(1)} %bitcast.85, s32[1024]{0:T(1024)S(1)} %add_select_fusion, s32[]{:T(128)} %constant.29.clone.1), kind=kCustom, calls=%fused_computation.41 | custom fusion | bytes 5124 | tf_op jit(solution)/shard_map/scatter | solution.py:31
  13.8 5.1 %gather_fusion = bf16[1280,1024]{1,0:T(8,128)(2,1)} fusion(bf16[128,1024]{1,0:T(8,128)(2,1)S(1)} %copy-done.1, s32[2048]{0:T(1024)S(1)} %pad_clamp_fusion), kind=kCustom, calls=%fused_computation | custom fusion | bytes 5248000 | tf_op jit(solution)/shard_map/gather | solution.py:37
  18.9 5.9 %gather.9 = bf16[128,10,1024]{2,1,0:T(8,128)(2,1)} reshape(bf16[1280,1024]{1,0:T(8,128)(2,1)} %gather_fusion) | data formatting | bytes 5242880 | tf_op jit(solution)/shard_map/gather | solution.py:37
  24.8 7.6 %scatter_custom_fusion.1 = bf16[1280]{0:T(1024)(128)(2,1)S(1)} fusion(s32[1024]{0:T(1024)S(1)} %bitcast.86, bf16[1024]{0:T(1024)(128)(2,1)S(1)} %broadcast.65, bf16[]{:T(256)} %constant.37.clone.1), kind=kCustom, calls=%fused_computation.45 | custom fusion | bytes 2562 | tf_op jit(solution)/shard_map/scatter | solution.py:35
  32.6 2.5 broadcast_multiply_fusion
  35.1 110.8 %all_to_all.15 = bf16[128,10,1024]{2,1,0:T(8,128)(2,1)S(1)} all-to-all(bf16[128,10,1024]{2,1,0:T(8,128)(2,1)S(1)} %broadcast_multiply_fusion), channel_id=1, replica_groups=mesh['ep'=128,'half'=2] {'ep'}, dimensions={0} | all-to-all | bytes 5242880 | tf_op jit(solution)/shard_map/all_to_all | solution.py:38
  145.9 2.9 copy.28
  148.9 17.1 %all-gather.2.cloned.1.call-done = bf16[128,10,2048]{2,0,1:T(8,128)(2,1)} async-done(((bf16[128,10,1024]{2,0,1:T(8,128)(2,1)}), bf16[128,10,2048]{2,0,1:T(8,128)(2,1)}) %all-gather.2.cloned.1.call-update) | async-done | bytes 5242896 | tf_op jit(solution)/shard_map/all_gather | solution.py:40
  166.0 7.1 %fusion.8 = f32[128,10,384]{2,0,1:T(8,128)} fusion(bf16[128,10,2048]{2,0,1:T(8,128)(2,1)} %all-gather.2.cloned.1.call-done, bf16[1,2048,384]{2,1,0:T(8,128)(2,1)} %param.9), kind=kOutput, calls=%fused_computation.18 | convolution fusion | flops 2013265920 | bytes 8781824 | tf_op jit(solution)/shard_map/secd,edf->secf/dot_general | solution.py:43
  173.1 9.8 %convolution_convert_fusion = bf16[128,10,2048]{2,0,1:T(8,128)(2,1)} fusion(bf16[1,384,2048]{2,1,0:T(8,128)(2,1)S(1)} %copy-done, bf16[128,10,2048]{2,0,1:T(8,128)(2,1)} %all-gather.2.cloned.1.call-done, bf16[1,2048,384]{2,1,0:T(8,128)(2,1)} %param.10, f32[128,10,384]{2,0,1:T(8,128)} %fusion.8), kind=kOutput, calls=%fused_computation.5 | convolution fusion | flops 4032102400 | bytes 15597568 | tf_op jit(solution)/shard_map/secf,efd->secd/dot_general | solution.py:46
  182.9 3.3 copy.38
  186.3 9.1 %all_to_all.16 = bf16[2,128,10,1024]{3,1,2,0:T(8,128)(2,1)} all-to-all(bf16[2,128,10,1024]{3,1,2,0:T(8,128)(2,1)S(1)} %bitcast.82), channel_id=1, replica_groups=mesh['ep'=128,'half'=2] {'half'}, dimensions={0} | all-to-all | bytes 10485760 | tf_op jit(solution)/shard_map/all_to_all | solution.py:15
  195.3 6.2 %reduce_sum.25 = bf16[128,10,1024]{2,0,1:T(8,128)(2,1)} reduce(bf16[2,128,10,1024]{3,1,2,0:T(8,128)(2,1)} %all_to_all.16, bf16[]{:T(256)} %constant.37.clone.1), dimensions={0}, to_apply=%region_5.6 | reduce | flops 1310720 | bytes 7864322 | tf_op jit(solution)/shard_map/reduce_sum | solution.py:16
  201.6 5.3 %copy.31 = bf16[128,10,1024]{2,1,0:T(8,128)(2,1)} copy(bf16[128,10,1024]{2,0,1:T(8,128)(2,1)} %reduce_sum.25) | data formatting | bytes 5242880 | tf_op jit(solution)/shard_map/reduce_sum | solution.py:16
  206.9 14.3 %all-to-all-start.2 = ((bf16[128,10,1024]{2,1,0:T(8,128)(2,1)}), bf16[128,10,1024]{2,1,0:T(8,128)(2,1)}, u32[]{:S(2)}, u32[]{:S(2)}) async-start(bf16[128,10,1024]{2,1,0:T(8,128)(2,1)} %copy.31), calls=%async_computation.2 | async-start | bytes 8388608 | tf_op jit(solution)/shard_map/all_to_all | solution.py:50
  221.4 96.1 %all-to-all-done.2 = bf16[128,10,1024]{2,1,0:T(8,128)(2,1)} async-done(((bf16[128,10,1024]{2,1,0:T(8,128)(2,1)}), bf16[128,10,1024]{2,1,0:T(8,128)(2,1)}, u32[]{:S(2)}, u32[]{:S(2)}) %all-to-all-start.2) | async-done | bytes 2621472 | tf_op jit(solution)/shard_map/all_to_all | solution.py:50
  317.5 6.1 %reshape.91 = bf16[1280,1024]{1,0:T(8,128)(2,1)} reshape(bf16[128,10,1024]{2,1,0:T(8,128)(2,1)} %all-to-all-done.2) | data formatting | bytes 5242880 | tf_op jit(solution)/shard_map/reshape | solution.py:51
  323.7 8.1 %gather_fusion.1 = bf16[1024,1024]{1,0:T(8,128)(2,1)} fusion(bf16[1280,1024]{1,0:T(8,128)(2,1)} %reshape.91, s32[1024]{0:T(1024)S(1)} %broadcast_clamp_fusion), kind=kCustom, calls=%fused_computation.1 | custom fusion | bytes 4198400 | tf_op jit(solution)/shard_map/gather | solution.py:51
  331.8 2.3 fusion
  334.1 0.8 copy.39
  (26 shorter events, 1.0 us)
Async XLA Ops:
  6.5 166.6 %copy-start = (bf16[1,384,2048]{2,1,0:T(8,128)(2,1)S(1)}, bf16[1,384,2048]{2,1,0:T(8,128)(2,1)}, u32[]{:S(2)}) copy-start(bf16[1,384,2048]{2,1,0:T(8,128)(2,1)} %param.11) | copy-start | bytes 4718596
  6.5 7.2 %copy-start.1 = (bf16[128,1024]{1,0:T(8,128)(2,1)S(1)}, bf16[128,1024]{1,0:T(8,128)(2,1)}, u32[]{:S(2)}) copy-start(bf16[128,1024]{1,0:T(8,128)(2,1)} %param.6) | copy-start | bytes 786436
  6.5 159.5 %all-gather.2.cloned.1.call-start = ((), (), s32[]{:S(2)}) async-start(), calls=%async_computation.3 | async-start | bytes 7864320 | tf_op jit(solution)/shard_map/all_gather | solution.py:40
  206.9 14.3 %copy-start.2 = (f32[128,8]{0,1:T(8,128)S(1)}, f32[128,8]{0,1:T(8,128)}, u32[]{:S(2)}) copy-start(f32[128,8]{0,1:T(8,128)} %param.7) | copy-start | bytes 12292
  206.9 110.6 %all-to-all-start.2 = ((bf16[128,10,1024]{2,1,0:T(8,128)(2,1)}), bf16[128,10,1024]{2,1,0:T(8,128)(2,1)}, u32[]{:S(2)}, u32[]{:S(2)}) async-start(bf16[128,10,1024]{2,1,0:T(8,128)(2,1)} %copy.31), calls=%async_computation.2 | async-start | bytes 8388608 | tf_op jit(solution)/shard_map/all_to_all | solution.py:50
Sparse Core Ops, SparseCore 0:
  149.0 16.9 all-gather.1
where the time goes:
time: 342 us
  blocking collectives  120 us (35%)
  waiting for transfers between devices  113 us (33%)
  local copies, waits for them, and re-layouts  51.4 us (15%)
  matrix products  19.2 us (6%)
  starting transfers between devices  14.3 us (4%)
  between operations  13.5 us (4%)
  other arithmetic  10.1 us (3%)
    all_to_all x1, blocking collectives, local(): lax.all_to_all(outgoing, 'ep', split_axis=0, concat_axis=0, tiled=True)  111 us
    all_to_all x1, waiting for transfers between devices, local(): lax.all_to_all(summed, 'ep', split_axis=0, concat_axis=0, tiled=True)  96.1 us
    all_gather x1, waiting for transfers between devices, local(): whole = lax.all_gather(received, 'half', axis=2, tiled=True)  17.1 us
    all_to_all x1, starting transfers between devices, local(): lax.all_to_all(summed, 'ep', split_axis=0, concat_axis=0, tiled=True)  14.3 us
    gather x2, local copies, waits for them, and re-layouts, local(): tokens[token_table] * filled[:, None]  11 us
    dot_general x1, matrix products, local(): jnp.einsum('secf,efd->secd', hidden, w_down, preferred_element_type=jnp.f...  9.81 us
    all_to_all x1, blocking collectives, summed_on_arrival(): blocks = lax.all_to_all(cut_along(value, dim, size), axis, 0, 0, tiled=True)  9.08 us
    gather x1, local copies, waits for them, and re-layouts, local(): answer.reshape(experts * capacity, -1)[slot].reshape(tok_dev, top, -1)  8.11 us
  transfers between devices with their start and end apart: 2, of which 2 were waited for; matrix products, arithmetic and copies ran while one was open for 0% of the time, Pallas kernels for 0%

commit v1 on v0

--- a/solution.py
+++ b/solution.py
@@ -37,7 +37,9 @@
     outgoing = (tokens[token_table] * filled[:, None]).reshape(experts, capacity, half_width)
     received = lax.all_to_all(outgoing, "ep", split_axis=0, concat_axis=0, tiled=True)
     count = received.shape[1]
-    whole = lax.all_gather(received, "half", axis=2, tiled=True)
+    whole = jnp.concatenate(
+        lax.all_to_all(jnp.stack([received] * lax.axis_size("half")), "half", 0, 0), axis=2
+    )
     width = whole.shape[2]
     grouped = whole.reshape(-1, local_experts, count, width)
     gate = jnp.einsum("secd,edf->secf", grouped, w_gate, preferred_element_type=jnp.float32)

time: 342 us -> 314 us (0.918)
  waiting for transfers between devices: 113 us -> 96.1 us
  between operations: 13.5 us -> 0.18 us
  blocking collectives: 120 us -> 128 us
  starting transfers between devices: 14.3 us -> 9.41 us
    all_gather x1 -> x0, waiting for transfers between devices: 17.1 us -> none  [local(): whole = lax.all_gather(received, 'half', axis=2, tiled=True)]
    all_to_all x0 -> x1, blocking collectives: none -> 7.95 us  [local(): lax.all_to_all(jnp.stack([received] * lax.axis_size('half')), 'half', 0, 0)]
    all_to_all x1, starting transfers between devices: 14.3 us -> 9.41 us  [local(): lax.all_to_all(summed, 'ep', split_axis=0, concat_axis=0, tiled=True)]
  transfers between devices with their start and end apart: 2 -> 1, of which waited for: 2 -> 1; matrix products, arithmetic and copies ran while one was open for 0% -> 0% of each run, Pallas kernels for 0% -> 0%
where the time goes in v1:
time: 314 us
  blocking collectives  128 us (41%)
  waiting for transfers between devices  96.1 us (31%)
  local copies, waits for them, and re-layouts  53.2 us (17%)
  matrix products  16.2 us (5%)
  other arithmetic  10.6 us (3%)
  starting transfers between devices  9.41 us (3%)
    all_to_all x1, blocking collectives, local(): lax.all_to_all(outgoing, 'ep', split_axis=0, concat_axis=0, tiled=True)  111 us
    all_to_all x1, waiting for transfers between devices, local(): lax.all_to_all(summed, 'ep', split_axis=0, concat_axis=0, tiled=True)  96.1 us
    gather x2, local copies, waits for them, and re-layouts, local(): tokens[token_table] * filled[:, None]  11 us
    dot_general x1, matrix products, local(): jnp.einsum('secf,efd->secd', hidden, w_down, preferred_element_type=jnp.f...  9.8 us
    all_to_all x1, starting transfers between devices, local(): lax.all_to_all(summed, 'ep', split_axis=0, concat_axis=0, tiled=True)  9.41 us
    all_to_all x1, blocking collectives, summed_on_arrival(): blocks = lax.all_to_all(cut_along(value, dim, size), axis, 0, 0, tiled=True)  9.08 us
    gather x1, local copies, waits for them, and re-layouts, local(): answer.reshape(experts * capacity, -1)[slot].reshape(tok_dev, top, -1)  8.23 us
    all_to_all x1, blocking collectives, local(): lax.all_to_all(jnp.stack([received] * lax.axis_size('half')), 'half', 0, 0)  7.95 us
  transfers between devices with their start and end apart: 1, of which 1 were waited for; matrix products, arithmetic and copies ran while one was open for 0% of the time, Pallas kernels for 0%

profile of v1, /device:TPU:24, one launch (start us, length us, event | category | flops | bytes accessed | tf_op | source)
XLA Modules:
  0.0 313.5 jit_solution(3097670013584744453)
XLA Ops:
  0.0 0.9 copy.26
  1.1 0.7 broadcast_multiply_fusion.1
  2.9 4.3 %scatter_custom_fusion = s32[1280]{0:T(1024)S(1)} fusion(s32[1024]{0:T(1024)S(1)} %bitcast.95, s32[1024]{0:T(1024)S(1)} %add_select_fusion, s32[]{:T(128)} %constant.29.clone.1), kind=kCustom, calls=%fused_computation.43 | custom fusion | bytes 5124 | tf_op jit(solution)/shard_map/scatter | solution.py:31
  7.3 5.1 %gather_fusion = bf16[1280,1024]{1,0:T(8,128)(2,1)} fusion(bf16[128,1024]{1,0:T(8,128)(2,1)S(1)} %copy-done.2, s32[2048]{0:T(1024)S(1)} %pad_clamp_fusion), kind=kCustom, calls=%fused_computation | custom fusion | bytes 5248000 | tf_op jit(solution)/shard_map/gather | solution.py:37
  12.3 5.9 %gather.9 = bf16[128,10,1024]{2,1,0:T(8,128)(2,1)} reshape(bf16[1280,1024]{1,0:T(8,128)(2,1)} %gather_fusion) | data formatting | bytes 5242880 | tf_op jit(solution)/shard_map/gather | solution.py:37
  18.3 7.6 %scatter_custom_fusion.1 = bf16[1280]{0:T(1024)(128)(2,1)S(1)} fusion(s32[1024]{0:T(1024)S(1)} %bitcast.96, bf16[1024]{0:T(1024)(128)(2,1)S(1)} %broadcast.65, bf16[]{:T(256)} %constant.37.clone.1), kind=kCustom, calls=%fused_computation.47 | custom fusion | bytes 2562 | tf_op jit(solution)/shard_map/scatter | solution.py:35
  26.0 2.5 broadcast_multiply_fusion
  28.6 110.8 %all_to_all.20 = bf16[128,10,1024]{2,1,0:T(8,128)(2,1)S(1)} all-to-all(bf16[128,10,1024]{2,1,0:T(8,128)(2,1)S(1)} %broadcast_multiply_fusion), channel_id=1, replica_groups=mesh['ep'=128,'half'=2] {'ep'}, dimensions={0} | all-to-all | bytes 5242880 | tf_op jit(solution)/shard_map/all_to_all | solution.py:38
  139.4 1.4 copy.44
  141.3 7.9 %all_to_all.21 = bf16[2,128,10,1024]{3,1,2,0:T(8,128)(2,1)S(1)} all-to-all(bf16[2,128,10,1024]{3,1,2,0:T(8,128)(2,1)S(1)} %pad_maximum_fusion), channel_id=1, replica_groups=mesh['ep'=128,'half'=2] {'half'}, dimensions={0} | all-to-all | bytes 10485760 | tf_op jit(solution)/shard_map/all_to_all | solution.py:41
  149.3 0.9 copy.39
  150.1 2.3 copy-done.3
  152.4 4.1 %fusion.8 = f32[128,10,384]{2,0,1:T(8,128)} fusion(bf16[128,10,2048]{2,0,1:T(8,128)(2,1)S(1)} %bitcast.91, bf16[1,2048,384]{2,1,0:T(8,128)(2,1)S(1)} %copy-done.5), kind=kOutput, calls=%fused_computation.20 | convolution fusion | flops 2013265920 | bytes 8781824 | tf_op jit(solution)/shard_map/secd,edf->secf/dot_general | solution.py:45
  156.6 9.8 %convolution_convert_fusion = bf16[128,10,2048]{2,0,1:T(8,128)(2,1)} fusion(bf16[1,384,2048]{2,1,0:T(8,128)(2,1)S(1)} %copy-done, bf16[128,10,2048]{2,0,1:T(8,128)(2,1)} %bitcast.92, bf16[1,2048,384]{2,1,0:T(8,128)(2,1)} %param.10, f32[128,10,384]{2,0,1:T(8,128)} %fusion.8), kind=kOutput, calls=%fused_computation.6 | convolution fusion | flops 4032102400 | bytes 15597568 | tf_op jit(solution)/shard_map/secf,efd->secd/dot_general | solution.py:48
  166.4 3.3 %copy.43 = bf16[10,16,2,8,1024]{4,3,1,0,2:T(8,128)(2,1)S(1)} copy(bf16[10,16,2,8,1024]{4,3,2,1,0:T(8,128)(2,1)} %bitcast.93) | data formatting | bytes 10485760 | tf_op jit(solution)/shard_map/reshape | solution.py:9
  169.7 9.1 %all_to_all.22 = bf16[2,128,10,1024]{3,1,2,0:T(8,128)(2,1)} all-to-all(bf16[2,128,10,1024]{3,1,2,0:T(8,128)(2,1)S(1)} %bitcast.89), channel_id=1, replica_groups=mesh['ep'=128,'half'=2] {'half'}, dimensions={0} | all-to-all | bytes 10485760 | tf_op jit(solution)/shard_map/all_to_all | solution.py:15
  178.8 6.2 %reduce_sum.25 = bf16[128,10,1024]{2,0,1:T(8,128)(2,1)} reduce(bf16[2,128,10,1024]{3,1,2,0:T(8,128)(2,1)} %all_to_all.22, bf16[]{:T(256)} %constant.37.clone.1), dimensions={0}, to_apply=%region_5.6 | reduce | flops 1310720 | bytes 7864322 | tf_op jit(solution)/shard_map/reduce_sum | solution.py:16
  185.0 5.3 %copy.34 = bf16[128,10,1024]{2,1,0:T(8,128)(2,1)} copy(bf16[128,10,1024]{2,0,1:T(8,128)(2,1)} %reduce_sum.25) | data formatting | bytes 5242880 | tf_op jit(solution)/shard_map/reduce_sum | solution.py:16
  190.4 9.4 %all-to-all-start.3 = ((bf16[128,10,1024]{2,1,0:T(8,128)(2,1)}), bf16[128,10,1024]{2,1,0:T(8,128)(2,1)}, u32[]{:S(2)}, u32[]{:S(2)}) async-start(bf16[128,10,1024]{2,1,0:T(8,128)(2,1)} %copy.34), calls=%async_computation.3 | async-start | bytes 8388608 | tf_op jit(solution)/shard_map/all_to_all | solution.py:52
  200.0 96.1 %all-to-all-done.3 = bf16[128,10,1024]{2,1,0:T(8,128)(2,1)} async-done(((bf16[128,10,1024]{2,1,0:T(8,128)(2,1)}), bf16[128,10,1024]{2,1,0:T(8,128)(2,1)}, u32[]{:S(2)}, u32[]{:S(2)}) %all-to-all-start.3) | async-done | bytes 2621472 | tf_op jit(solution)/shard_map/all_to_all | solution.py:52
  296.1 6.1 %reshape.97 = bf16[1280,1024]{1,0:T(8,128)(2,1)} reshape(bf16[128,10,1024]{2,1,0:T(8,128)(2,1)} %all-to-all-done.3) | data formatting | bytes 5242880 | tf_op jit(solution)/shard_map/reshape | solution.py:53
  302.2 8.2 %gather_fusion.1 = bf16[1024,1024]{1,0:T(8,128)(2,1)} fusion(bf16[1280,1024]{1,0:T(8,128)(2,1)} %reshape.97, s32[1024]{0:T(1024)S(1)} %broadcast_clamp_fusion), kind=kCustom, calls=%fused_computation.1 | custom fusion | bytes 4198400 | tf_op jit(solution)/shard_map/gather | solution.py:53
  310.5 2.3 fusion
  312.8 0.8 copy.45
  (32 shorter events, 2.0 us)
Async XLA Ops:
  0.0 156.6 %copy-start = (bf16[1,384,2048]{2,1,0:T(8,128)(2,1)S(1)}, bf16[1,384,2048]{2,1,0:T(8,128)(2,1)}, u32[]{:S(2)}) copy-start(bf16[1,384,2048]{2,1,0:T(8,128)(2,1)} %param.11) | copy-start | bytes 4718596
  0.0 7.2 %copy-start.2 = (bf16[128,1024]{1,0:T(8,128)(2,1)S(1)}, bf16[128,1024]{1,0:T(8,128)(2,1)}, u32[]{:S(2)}) copy-start(bf16[128,1024]{1,0:T(8,128)(2,1)} %param.6) | copy-start | bytes 786436
  149.3 3.2 %copy-start.5 = (bf16[1,2048,384]{2,1,0:T(8,128)(2,1)S(1)}, bf16[1,2048,384]{2,1,0:T(8,128)(2,1)}, u32[]{:S(2)}) copy-start(bf16[1,2048,384]{2,1,0:T(8,128)(2,1)} %param.9) | copy-start | bytes 4718596
  150.1 2.3 copy-start.3
  190.4 9.4 %copy-start.4 = (f32[128,8]{0,1:T(8,128)S(1)}, f32[128,8]{0,1:T(8,128)}, u32[]{:S(2)}) copy-start(f32[128,8]{0,1:T(8,128)} %param.7) | copy-start | bytes 12292
  190.4 105.7 %all-to-all-start.3 = ((bf16[128,10,1024]{2,1,0:T(8,128)(2,1)}), bf16[128,10,1024]{2,1,0:T(8,128)(2,1)}, u32[]{:S(2)}, u32[]{:S(2)}) async-start(bf16[128,10,1024]{2,1,0:T(8,128)(2,1)} %copy.34), calls=%async_computation.3 | async-start | bytes 8388608 | tf_op jit(solution)/shard_map/all_to_all | solution.py:52
  302.2 11.3 %copy-start.1 = (bf16[1,384,2048]{2,1,0:T(8,128)(2,1)S(1)}, bf16[1,384,2048]{2,1,0:T(8,128)(2,1)}, u32[]{:S(2)}) copy-start(bf16[1,384,2048]{2,1,0:T(8,128)(2,1)} %param.11) | copy-start | bytes 4718596
